TPU v7x, 32 devices: a whole 2x2x4 slice. The times are simulated.
32 devices in a mesh: row: 2 (over x), col: 16 (over z, y, core).
Axes of the slice: x: 2, y: 2, z: 4, core: 2. Of those that a mesh axis runs over, the one named last changes fastest.
Arguments:
- adjacency: int32 [2048, 64], P('row', 'col'), may hold values from -2147483648 to 2147483647, as said below
- tile_mask: int32 [16, 16], P('row', 'col'), may hold values from 0 to 1, as said below
- thresholds: int32 [3], replicated, may hold values from 30 to 61
Outputs:
- truss_support: float32 [2048, 2048], P('row', 'col')
- edge_counts: int32 [3], replicated
Inputs may be any that keep to these rules, and one draw needn't show every extreme that they name: The graph of adjacency is symmetric with an empty diagonal: bit b of word w of row i equals the bit for row 32 w + b and column i. `tile_mask`: Symmetric.
All inputs are finite; a program needn't handle non-finite values.
Results may differ from a plain program's by a relative error of at most 0.0003.
Values may be sent and summed in bfloat16 or wider, within the bound.
A program may use at most 64 MiB of HBM per device.

v0:
```python
import jax
import jax.numpy as jnp
from jax import lax
from jax.sharding import PartitionSpec as P

TILE = 128
ITERS = 3


def unpack_bits(packed_rows):
    shifts = jnp.arange(32, dtype=jnp.int32)
    flat_bits = jnp.bitwise_and(jnp.right_shift(packed_rows[:, :, None], shifts), 1)
    return flat_bits.reshape(packed_rows.shape[0], packed_rows.shape[1] * 32)


def pack_bits(flat_bits):
    shifts = jnp.arange(32, dtype=jnp.int32)
    grouped = flat_bits.reshape(flat_bits.shape[0], flat_bits.shape[1] // 32, 32)
    return jnp.sum(jnp.left_shift(grouped, shifts), axis=-1, dtype=jnp.int32)


def block_product(packed_rows, matching):
    operand = unpack_bits(packed_rows).astype(jnp.bfloat16)
    return jnp.dot(operand, matching, preferred_element_type=jnp.float32)


def local(adjacency, tile_mask, thresholds):
    rows_here = adjacency.shape[0]
    cols_here = adjacency.shape[1] * 32
    flat_bits = unpack_bits(adjacency)
    tile_cover = jnp.broadcast_to(
        tile_mask[:, None, :, None], (tile_mask.shape[0], TILE, tile_mask.shape[1], TILE)
    )
    surviving = flat_bits * tile_cover.reshape(rows_here, cols_here)
    survived_list = []
    support = jnp.zeros((rows_here, cols_here), jnp.float32)
    for iteration in range(ITERS):
        packed_here = pack_bits(surviving)
        column_words = lax.all_gather(packed_here, "row", axis=0, tiled=True)
        column_bits = unpack_bits(column_words)
        lower_panel = column_bits.astype(jnp.bfloat16)
        wedge_counts = block_product(
            lax.all_gather(packed_here, "col", axis=1, tiled=True), lower_panel
        )
        support = wedge_counts * surviving.astype(jnp.float32)
        retained = (support >= thresholds[iteration].astype(jnp.float32)).astype(jnp.int32)
        surviving = surviving * retained
        survived = jnp.sum(surviving)
        survived_list.append(survived)
    edge_counts = lax.psum(jnp.stack(survived_list), ("row", "col"))
    truss_support = (
        support * surviving.astype(jnp.float32) / thresholds[ITERS - 1].astype(jnp.float32)
    )
    return (truss_support, edge_counts)


def solution(mesh):
    in_specs = (P("row", "col"), P("row", "col"), P())
    out_specs = (P("row", "col"), P())
    return jax.shard_map(local, mesh=mesh, in_specs=in_specs, out_specs=out_specs, check_vma=False)
```

profile of v0, /device:TPU:0, one launch (start us, length us, event | category | flops | bytes accessed | tf_op | source)
XLA Modules:
  0.0 130.6 jit_solution(8113006497730622411)
XLA Ops:
  0.6 0.0 copy-start
  0.6 0.6 copy-done
  1.3 1.3 %fusion.8 = (s32[1]{0:T(128)}, s32[1]{0:T(128)}, s32[1]{0:T(128)}) fusion(s32[3]{0:T(128)} %param.5), kind=kLoop, calls=%fused_computation.25 | loop fusion | bytes 24 | tf_op jit(solution)/shard_map/slice | solution.py:46
  4.5 0.1 shift_right_arithmetic.170
  4.6 0.1 broadcast_bitcast_fusion
  4.7 0.8 shift-left_reduce_fusion.2
  5.5 5.3 %all_gather.19 = s32[2048,4]{0,1:T(4,128)S(1)} all-gather(s32[1024,4]{0,1:T(4,128)S(1)} %shift-left_reduce_fusion.2), channel_id=1, replica_groups=mesh['row'=2,'col'=16] {'row'}, dimensions={0}, use_global_device_ids=true | all-gather | bytes 49152 | tf_op jit(solution)/shard_map/all_gather | solution.py:39
  10.8 22.9 %all-gather = s32[16,4,1024]{2,1,0:T(4,128)S(1)} all-gather(s32[1,4,1024]{2,1,0:T(4,128)S(1)} %bitcast.55), channel_id=1, replica_groups=mesh['row'=2,'col'=16] {'col'}, dimensions={0}, use_global_device_ids=true | all-gather | bytes 278528 | tf_op jit(solution)/shard_map/all_gather | solution.py:43
  33.7 0.1 reshape.241
  33.8 0.1 and_convert_fusion.5
  34.0 0.8 fusion.5
  34.8 1.6 %and_convert_fusion.2 = bf16[1024,64,32]{0,2,1:T(8,128)(2,1)S(1)} fusion(s32[1024,64]{0,1:T(8,128)S(1)} %bitcast.49), kind=kLoop, calls=%fused_computation.2 | loop fusion | flops 6291456 | bytes 4456448 | tf_op jit(solution)/shard_map/convert_element_type | solution.py:23
  36.4 0.9 shift-left_reduce_fusion.1
  37.3 0.8 reduce_sum.57
  38.0 4.4 %all_gather.21 = s32[2048,4]{0,1:T(4,128)S(1)} all-gather(s32[1024,4]{0,1:T(4,128)S(1)} %get-tuple-element.13), channel_id=1, replica_groups=mesh['row'=2,'col'=16] {'row'}, dimensions={0}, use_global_device_ids=true | all-gather | bytes 49152 | tf_op jit(solution)/shard_map/all_gather | solution.py:39
  42.4 17.8 %all-gather.1 = s32[16,4,1024]{2,1,0:T(4,128)S(1)} all-gather(s32[1,4,1024]{2,1,0:T(4,128)S(1)} %bitcast.53), channel_id=1, replica_groups=mesh['row'=2,'col'=16] {'col'}, dimensions={0}, use_global_device_ids=true | all-gather | bytes 278528 | tf_op jit(solution)/shard_map/all_gather | solution.py:43
  60.3 0.1 reshape.243
  60.3 0.1 and_convert_fusion.4
  60.5 1.6 %and_convert_fusion.1 = bf16[1024,64,32]{0,2,1:T(8,128)(2,1)S(1)} fusion(s32[1024,64]{0,1:T(8,128)S(1)} %bitcast.50), kind=kLoop, calls=%fused_computation.1 | loop fusion | flops 6291456 | bytes 4456448 | tf_op jit(solution)/shard_map/convert_element_type | solution.py:23
  62.0 0.9 shift-left_reduce_fusion
  63.0 4.4 %all_gather.23 = s32[2048,4]{0,1:T(4,128)S(1)} all-gather(s32[1024,4]{0,1:T(4,128)S(1)} %get-tuple-element.15), channel_id=1, replica_groups=mesh['row'=2,'col'=16] {'row'}, dimensions={0}, use_global_device_ids=true | all-gather | bytes 49152 | tf_op jit(solution)/shard_map/all_gather | solution.py:39
  67.4 19.9 %all-gather.2 = s32[16,4,1024]{2,1,0:T(4,128)S(1)} all-gather(s32[1,4,1024]{2,1,0:T(4,128)S(1)} %bitcast.54), channel_id=1, replica_groups=mesh['row'=2,'col'=16] {'col'}, dimensions={0}, use_global_device_ids=true | all-gather | bytes 278528 | tf_op jit(solution)/shard_map/all_gather | solution.py:43
  87.3 0.1 reshape.245
  87.4 0.1 and_convert_fusion.3
  87.5 1.6 %and_convert_fusion = bf16[1024,64,32]{0,2,1:T(8,128)(2,1)S(1)} fusion(s32[1024,64]{0,1:T(8,128)S(1)} %bitcast.51), kind=kLoop, calls=%fused_computation | loop fusion | flops 6291456 | bytes 4456448 | tf_op jit(solution)/shard_map/convert_element_type | solution.py:23
  89.1 0.9 multiply_divide_fusion
  89.9 0.9 fusion.7
  90.8 2.0 %pad_add_fusion = s32[3]{0:T(128)S(1)} fusion(s32[1]{0:T(128)} %bitcast.25, s32[1]{0:T(128)} %bitcast.24, s32[1]{0:T(128)} %bitcast.23), kind=kLoop, calls=%fused_computation.23 | loop fusion | flops 6 | bytes 24 | tf_op jit(solution)/shard_map/stack | solution.py:50
  92.8 1.0 copy.11
  93.8 36.8 %psum.7 = s32[3]{0:T(128)} all-reduce(s32[3]{0:T(128)S(1)} %pad_add_fusion), channel_id=1, replica_groups=mesh['row'=2,'col'=16] {'row','col'}, use_global_device_ids=true, to_apply=%region_6.0 | all-reduce | flops 3 | bytes 24 | tf_op jit(solution)/shard_map/psum | solution.py:50
  (1 shorter events, 0.0 us)
Async XLA Ops:
  0.6 0.7 copy-start
where the time goes:
time: 132 us; the launch traced here: 131 us
  blocking collectives  112 us (85%)
  other arithmetic  10.3 us (8%)
  local copies, waits for them, and re-layouts  3.42 us (3%)
  matrix products  2.67 us (2%)
  between operations  2.59 us (2%)
    all_gather x3, blocking collectives, local(): lax.all_gather(packed_here, 'col', axis=1, tiled=True)  60.6 us
    psum x1, blocking collectives, local(): edge_counts = lax.psum(jnp.stack(survived_list), ('row', 'col'))  36.8 us
    all_gather x3, blocking collectives, local(): column_words = lax.all_gather(packed_here, 'row', axis=0, tiled=True)  14.1 us
    convert_element_type x3, other arithmetic, block_product(): operand = unpack_bits(packed_rows).astype(jnp.bfloat16)  4.67 us
    dot_general x3, matrix products, block_product(): return jnp.dot(operand, matching, preferred_element_type=jnp.float32)  2.67 us

commit v1 on v0

v1 whole, which is shorter than its diff:
```python
import functools

import jax
import jax.numpy as jnp
from jax import lax
from jax.experimental import pallas as pl
from jax.experimental.pallas import tpu as pltpu
from jax.sharding import PartitionSpec as P

TILE = 128
ITERS = 3
BITS = 32
MESH = pl.DeviceIdType.MESH


def unpack_words(load_row, words, width, dtype):
    bit = lax.broadcasted_iota(jnp.int32, (BITS, width), 0)
    parts = []
    for w in range(words):
        row = jnp.broadcast_to(load_row(w), (BITS, width))
        parts.append(jnp.bitwise_and(jnp.right_shift(row, bit), 1).astype(jnp.float32).astype(dtype))
    return parts


def kernel(
    n_row, n_col, adj_ref, mask_ref, thr_ref, out_ref, count_ref,
    gath, cross, lhs, rhs, acc, live, tally, tallies,
    send_a, recv_a, send_f, recv_f, send_x, recv_x, send_c, recv_c,
):
    words, rows = adj_ref.shape
    cols = words * BITS
    pairs = n_col // 2
    n_dev = n_row * n_col
    my_row, my_col = lax.axis_index("row"), lax.axis_index("col")
    my_pair, my_core = my_col // 2, lax.rem(my_col, 2)
    me = my_row * n_col + my_col
    tiles_here = rows // TILE

    def device(flat):
        return (flat // n_col, lax.rem(flat, n_col))

    barrier = pltpu.get_barrier_semaphore()

    def greet(d, c):
        pl.semaphore_signal(
            barrier, inc=1, device_id=device(lax.rem(me + d, n_dev)), device_id_type=MESH
        )
        return c

    lax.fori_loop(1, n_dev, greet, 0)

    def keep_own(t, w, value):
        gath[t, my_col, w : w + 1, :] = value
        cross[t, my_row, w : w + 1, :] = value

    for w in range(words):
        keep_own(
            0, w,
            jnp.concatenate(
                [adj_ref[w : w + 1, i * TILE : (i + 1) * TILE] * mask_ref[i, 0] for i in range(tiles_here)],
                axis=1,
            ),
        )
    tally[...] = jnp.zeros_like(tally)
    pl.semaphore_wait(barrier, n_dev - 1)

    def direct(t, d):
        return pltpu.make_async_remote_copy(
            src_ref=gath.at[t, my_col], dst_ref=gath.at[t, my_col],
            send_sem=send_a.at[t, d], recv_sem=recv_a.at[t, d],
            device_id=(my_row, lax.rem(my_pair + d, pairs) * 2 + my_core), device_id_type=MESH,
        )

    def forward(t, d):
        slot = lax.rem(my_pair - d + pairs, pairs) * 2 + my_core
        return pltpu.make_async_remote_copy(
            src_ref=gath.at[t, slot], dst_ref=gath.at[t, slot],
            send_sem=send_f.at[t, d], recv_sem=recv_f.at[t, d],
            device_id=(my_row, my_pair * 2 + 1 - my_core), device_id_type=MESH,
        )

    def across(t, d):
        return pltpu.make_async_remote_copy(
            src_ref=gath.at[t, my_col], dst_ref=cross.at[t, my_row],
            send_sem=send_x.at[t, d], recv_sem=recv_x.at[t, d],
            device_id=(lax.rem(my_row + d, n_row), my_col), device_id_type=MESH,
        )

    def distance(k):
        odd = lax.rem(k, 2)
        return odd * ((k + 1) // 2) + (1 - odd) * (pairs - k // 2)

    def multiply(t, d):
        pair = lax.rem(my_pair - d + pairs, pairs)
        for core in range(2):
            slot = pair * 2 + core
            parts = unpack_words(lambda w: gath[t, slot, w : w + 1, :], words, rows, jnp.bfloat16)
            for w in range(words):
                rhs[core * cols + w * BITS : core * cols + (w + 1) * BITS, :] = parts[w]
        return jnp.dot(lhs[pair], rhs[...], preferred_element_type=jnp.float32)

    for t in range(ITERS):
        threshold = thr_ref[t].astype(jnp.float32)
        for d in range(1, n_row):
            across(t, d).start()
        forward(t, 0).start()

        def send(k, c):
            direct(t, distance(pairs - k)).start()
            return c

        lax.fori_loop(1, pairs, send, 0)

        parts = unpack_words(lambda w: gath[t, my_col, w : w + 1, :], words, rows, jnp.float32)
        for w in range(words):
            live[w * BITS : (w + 1) * BITS, :] = parts[w]
        for d in range(1, n_row):
            across(t, d).wait_recv()
        wide = 2 * cols
        for r in range(n_row):
            parts = unpack_words(lambda w: cross[t, r, w : w + 1, :], words, rows, jnp.bfloat16)
            for w in range(words):
                for q in range(rows // wide):
                    lhs[r * (rows // wide) + q, w * BITS : (w + 1) * BITS, :] = parts[w][:, q * wide : (q + 1) * wide]

        def arrive(k):
            d = distance(k)
            direct(t, d).wait_recv()
            forward(t, d).start()

        arrive(1)
        forward(t, 0).wait_recv()
        acc[...] = multiply(t, 0)

        def step(k, c):
            arrive(k + 1)
            forward(t, distance(k)).wait_recv()
            acc[...] += multiply(t, distance(k))
            return c

        lax.fori_loop(1, pairs - 1, step, 0)
        forward(t, distance(pairs - 1)).wait_recv()
        acc[...] += multiply(t, distance(pairs - 1))

        support = acc[...] * live[...]
        kept = jnp.where(support >= threshold, live[...], 0.0)
        if t < ITERS - 1:
            bit = jnp.left_shift(1, lax.broadcasted_iota(jnp.int32, (BITS, rows), 0))
            for w in range(words):
                own = kept[w * BITS : (w + 1) * BITS, :].astype(jnp.int32) * bit
                keep_own(t + 1, w, jnp.sum(own, axis=0, keepdims=True))
        per_row = jnp.sum(kept, axis=0, keepdims=True)
        lanes = per_row[:, :TILE]
        for i in range(1, tiles_here):
            lanes = lanes + per_row[:, i * TILE : (i + 1) * TILE]
        tally[t : t + 1, :] = lanes.astype(jnp.int32)

    def count(d):
        return pltpu.make_async_remote_copy(
            src_ref=tally, dst_ref=tallies.at[me],
            send_sem=send_c.at[d], recv_sem=recv_c.at[d],
            device_id=device(lax.rem(me + d, n_dev)), device_id_type=MESH,
        )

    def send_count(d, c):
        count(n_dev - d).start()
        return c

    lax.fori_loop(1, n_dev, send_count, 0)
    tallies[me] = tally[...]
    ratio = support * kept / threshold
    for i in range(tiles_here):
        out_ref[i * TILE : (i + 1) * TILE, :] = ratio[:, i * TILE : (i + 1) * TILE].T

    def finish_count(d, c):
        count(d).wait()
        return c

    for t in range(ITERS):
        for d in range(1, n_row):
            across(t, d).wait_send()
        forward(t, 0).wait_send()

        def finish(d, c):
            direct(t, d).wait_send()
            forward(t, d).wait_send()
            return c

        lax.fori_loop(1, pairs, finish, 0)
    lax.fori_loop(1, n_dev, finish_count, 0)
    total = jnp.sum(tallies[...], axis=0)
    for t in range(ITERS):
        count_ref[t] = jnp.sum(total[t : t + 1, :])


def local(n_row, n_col, adjacency, tile_mask, thresholds):
    packed = adjacency.T
    words, rows = packed.shape
    cols = words * BITS
    n_dev = n_row * n_col
    pairs = n_col // 2
    dma = pltpu.SemaphoreType.DMA
    return pl.pallas_call(
        functools.partial(kernel, n_row, n_col),
        out_shape=(
            jax.ShapeDtypeStruct((rows, cols), jnp.float32),
            jax.ShapeDtypeStruct((ITERS,), jnp.int32),
        ),
        in_specs=[
            pl.BlockSpec(memory_space=pltpu.VMEM),
            pl.BlockSpec(memory_space=pltpu.SMEM),
            pl.BlockSpec(memory_space=pltpu.SMEM),
        ],
        out_specs=(
            pl.BlockSpec(memory_space=pltpu.VMEM),
            pl.BlockSpec(memory_space=pltpu.SMEM),
        ),
        scratch_shapes=[
            pltpu.VMEM((ITERS, n_col, words, rows), jnp.int32),
            pltpu.VMEM((ITERS, n_row, words, rows), jnp.int32),
            pltpu.VMEM((pairs, cols, 2 * cols), jnp.bfloat16),
            pltpu.VMEM((2 * cols, rows), jnp.bfloat16),
            pltpu.VMEM((cols, rows), jnp.float32),
            pltpu.VMEM((cols, rows), jnp.float32),
            pltpu.VMEM((8, TILE), jnp.int32),
            pltpu.VMEM((n_dev, 8, TILE), jnp.int32),
            dma((ITERS, pairs)), dma((ITERS, pairs)),
            dma((ITERS, pairs)), dma((ITERS, pairs)),
            dma((ITERS, n_row)), dma((ITERS, n_row)),
            dma((n_dev,)), dma((n_dev,)),
        ],
        compiler_params=pltpu.CompilerParams(collective_id=0, has_side_effects=True),
    )(packed, tile_mask, thresholds)


def solution(mesh):
    in_specs = (P("row", "col"), P("row", "col"), P())
    out_specs = (P("row", "col"), P())
    body = functools.partial(local, mesh.shape["row"], mesh.shape["col"])
    return jax.shard_map(body, mesh=mesh, in_specs=in_specs, out_specs=out_specs, check_vma=False)
```

time: 132 us -> 50.5 us (0.38)
  blocking collectives: 112 us -> 0 us
  Pallas kernels: 0 us -> 45.9 us
  other arithmetic: 10.3 us -> 0 us
  matrix products: 2.67 us -> 0 us
  between operations: 2.59 us -> 0.66 us
    all_gather x6 -> x0, blocking collectives: 74.7 us -> none  [the longest x3 60.6 us: local(): lax.all_gather(packed_here, 'col', axis=1, tiled=True)]
    pallas_call x0 -> x1, Pallas kernels: none -> 45.9 us  [local(): pl.pallas_call(functools.partial(kernel, n_row, n_col), out_shape=(jax.Sh...]
    psum x1 -> x0, blocking collectives: 36.8 us -> none  [local(): edge_counts = lax.psum(jnp.stack(survived_list), ('row', 'col'))]
    convert_element_type x6 -> x0, other arithmetic: 5.05 us -> none  [the longest x3 4.67 us: block_product(): operand = unpack_bits(packed_rows).astype(jnp.bfloat16)]
    dot_general x3 -> x0, matrix products: 2.67 us -> none  [block_product(): return jnp.dot(operand, matching, preferred_element_type=jnp.float32)]
    reduce_sum x3 -> x0, other arithmetic: 2.48 us -> none  [the longest x2 1.64 us: local(): survived = jnp.sum(surviving)]
    another operation x1 -> x0, other arithmetic: 1.97 us -> none  [local(): edge_counts = lax.psum(jnp.stack(survived_list), ('row', 'col'))]
    unnamed x6 -> x7, local copies, waits for them, and re-layouts: 1.92 us -> 3.7 us
where the time goes in v1:
time: 50.5 us; the launch traced here: 50.3 us
  Pallas kernels  45.9 us (91%)
  local copies, waits for them, and re-layouts  3.7 us (7%)
  between operations  0.66 us (1%)
    pallas_call x1, Pallas kernels, local(): pl.pallas_call(functools.partial(kernel, n_row, n_col), out_shape=(jax.Sh...  45.9 us
    unnamed x7, local copies, waits for them, and re-layouts  3.7 us

profile of v1, /device:TPU:0, one launch (start us, length us, event | category | flops | bytes accessed | tf_op | source)
XLA Modules:
  0.0 50.3 jit_solution(16396060705200313987)
XLA Ops:
  0.6 0.0 copy-start
  0.6 0.6 %copy-done = s32[8,1]{0,1:T(1,128)S(1)} copy-done((s32[8,1]{0,1:T(1,128)S(1)}, s32[8,1]{0,1:T(1,128)}, u32[]{:S(2)}) %copy-start) | copy-done | bytes 56
  1.3 0.7 %copy.5.mask_ref = s32[8,1]{1,0:T(8,128)} copy(s32[8,1]{0,1:T(1,128)S(1)} %copy-done) | data formatting | bytes 64 | tf_op args[1]
  2.0 45.9 %shard_map.50 = (f32[1024,128]{1,0:T(8,128)}, s32[3]{0:T(128)}) custom-call(s32[4,1024]{1,0:T(4,128)} %bitcast.1, s32[8,1]{1,0:T(8,128)} %copy.5.mask_ref, s32[3]{0:T(128)} %thr_ref.1), custom_call_target="tpu_custom_call" | custom-call | tf_op jit(solution)/shard_map/pallas_call | solution.py:203
  47.9 0.0 copy-start.1
  47.9 1.9 %copy.8 = f32[1024,128]{1,0:T(8,128)} copy(f32[1024,128]{1,0:T(8,128)} %get-tuple-element.4) | data formatting | bytes 1048576
  49.8 0.0 copy-done.1
  49.8 0.5 %copy.9 = s32[3]{0:T(128)} copy(s32[3]{0:T(128)S(1)} %copy-done.1) | data formatting | bytes 24
Async XLA Ops:
  0.6 0.7 %copy-start = (s32[8,1]{0,1:T(1,128)S(1)}, s32[8,1]{0,1:T(1,128)}, u32[]{:S(2)}) copy-start(s32[8,1]{0,1:T(1,128)} %param.4) | copy-start | bytes 100
  47.9 1.9 %copy-start.1 = (s32[3]{0:T(128)S(1)}, s32[3]{0:T(128)}, u32[]{:S(2)}) copy-start(s32[3]{0:T(128)} %get-tuple-element.5) | copy-start | bytes 40
